TPU v7x, 256 devices: a whole 4x4x8 slice. The times are simulated.
256 devices in a mesh: query: 8 (over y, z_hi), ctx: 32 (over x, z_lo, core).
Axes of the slice: x: 4, y: 4, z: 8 (z_hi: 2, z_lo: 4; z = z_hi * 4 + z_lo), core: 2. Of those that a mesh axis runs over, the one named last changes fastest.
Arguments:
- query_states: bfloat16 [256, 3072], P('query'), may hold values from -370 to 370
- key_states: bfloat16 [32768, 3072], P('ctx', 'query'), may hold values from -10.5 to 10.5
- value_states: bfloat16 [32768, 3072], P('ctx', 'query'), may hold values from -6 to 6
- level_ids: int32 [32768], P('ctx'), may hold values from 0 to 4, as said below
- level_bias: float32 [5, 24], replicated, may hold values from -1.5 to 1.5
- live_counts: int32 [32], P('ctx'), may hold values from 256 to 1024, as said below
- out_grad: bfloat16 [256, 3072], P('query'), may hold values from -6 to 6
Outputs:
- attn_out: bfloat16 [256, 3072], P(('query', 'ctx'))
- query_grad: bfloat16 [256, 3072], P(('query', 'ctx'))
- key_grad: bfloat16 [32768, 3072], P('ctx', 'query')
- value_grad: bfloat16 [32768, 3072], P('ctx', 'query')
Inputs may be any that keep to these rules, and one draw needn't show every extreme that they name: Owner c's slots c * 1024 to c * 1024 + live_counts[c] - 1 are live, its other slots are empty; at least one owner has all 1024 slots live. `level_ids`: constant over each aligned run of 16 slots.
All inputs are finite; a program needn't handle non-finite values.
Results may differ from a plain program's by a relative error of at most 0.012.
Values may be sent and summed in bfloat16 or wider, within the bound.
A program may use at most 64 MiB of HBM per device.

v0:
```python
import math
import jax
import jax.numpy as jnp
from jax import lax
from jax.sharding import PartitionSpec as P


def copy_for_each(x, axis):
    copies = jnp.broadcast_to(x, (lax.axis_size(axis), *x.shape))
    return lax.all_to_all(copies, axis, split_axis=0, concat_axis=0, tiled=True)


def over_copies(x, axis):
    return copy_for_each(x, axis).max(axis=0)


def split_up(x, dim, peers):
    dims = x.shape
    pieces = x.reshape(*dims[:dim], peers, dims[dim] // peers, *dims[dim + 1 :])
    return jnp.moveaxis(pieces, dim, 0)


def sum_at_owner(x, axis, dim):
    peers = lax.axis_size(axis)
    pieces = lax.all_to_all(split_up(x, dim, peers), axis, 0, 0, tiled=True)
    return jnp.sum(pieces, axis=0)


def gather_turned(arrays, axis, dims):
    turned = [jnp.moveaxis(a, dim, 0) for a, dim in zip(arrays, dims)]
    widths = [t[0].size for t in turned]
    both = jnp.concatenate([t.reshape(-1, w) for t, w in zip(turned, widths)], axis=1)
    out = lax.all_gather(both, axis, axis=0, tiled=True)
    pieces = jnp.split(out, [sum(widths[:k]) for k in range(1, len(widths))], axis=1)
    return tuple(
        (
            jnp.moveaxis(b.reshape(-1, *t.shape[1:]), 0, dim)
            for b, t, dim in zip(pieces, turned, dims)
        )
    )


def rescale(outputs, factor):
    row_count = outputs.shape[0]
    head_count = factor.shape[0]
    return (outputs.reshape(row_count, head_count, -1) * factor.T[:, :, None]).reshape(
        row_count, -1
    )


def local(query_states, key_states, value_states, level_ids, level_bias, live_counts, out_grad):
    query_ways = lax.axis_size("query")
    owner_ways = lax.axis_size("ctx")
    level_count, head_total = level_bias.shape
    moved_queries, moved_grads = (
        lax.all_to_all(query_states, "query", split_axis=1, concat_axis=0, tiled=True),
        lax.all_to_all(out_grad, "query", split_axis=1, concat_axis=0, tiled=True),
    )
    rows_total = moved_queries.shape[0]
    part_rows = rows_total // query_ways // owner_ways

    def regroup(array):
        return jnp.transpose(
            array.reshape(query_ways, owner_ways, part_rows, -1), (1, 0, 2, 3)
        ).reshape(rows_total, -1)

    queries_in = regroup(moved_queries)
    grads_in = regroup(moved_grads)
    key_full, value_full = (key_states, value_states)
    head_count = head_total // query_ways
    bias_table = lax.dynamic_slice_in_dim(
        level_bias, lax.axis_index("query") * head_count, head_count, 1
    )
    query_count, feature_count = queries_in.shape
    slot_count = key_full.shape[0]
    head_size = feature_count // head_count
    softmax_scale = 1.0 / math.sqrt(head_size)
    queries = queries_in.reshape(query_count, head_count, head_size)
    key_heads = key_full.reshape(slot_count, head_count, head_size)
    value_heads = value_full.reshape(slot_count, head_count, head_size)
    grad_heads = grads_in.reshape(query_count, head_count, head_size)
    live_slots = lax.broadcasted_iota(jnp.int32, (slot_count,), 0) < live_counts[0]
    level_onehot = (
        level_ids[:, None] == lax.broadcasted_iota(jnp.int32, (1, level_count), 1)
    ).astype(jnp.float32)
    level_term = jnp.dot(
        level_onehot,
        bias_table,
        precision=lax.Precision.HIGHEST,
        preferred_element_type=jnp.float32,
    )
    scores = (
        jnp.einsum("qhd,khd->hqk", queries, key_heads, preferred_element_type=jnp.float32)
        * softmax_scale
    )
    scores = jnp.where(live_slots[None, None, :], scores + level_term.T[:, None, :], -1e30)
    local_max = jnp.max(scores, axis=2)
    raw_weights = jnp.exp(scores - local_max[..., None])
    local_sum = jnp.sum(raw_weights, axis=2)
    partial_value = jnp.einsum(
        "hqk,khd->qhd",
        raw_weights.astype(jnp.bfloat16),
        value_heads,
        preferred_element_type=jnp.float32,
    ).reshape(query_count, feature_count)
    row_count = query_count // owner_ways
    row_start = lax.axis_index("ctx") * row_count
    row_peak = over_copies(local_max, "ctx")
    factor = jnp.exp(local_max - row_peak)
    out_rows, sum_rows = (
        sum_at_owner(rescale(partial_value, factor), "ctx", 0),
        sum_at_owner(local_sum * factor, "ctx", 1),
    )
    peak_rows = lax.dynamic_slice_in_dim(row_peak, row_start, row_count, 1)
    attention_rows = out_rows.reshape(row_count, head_count, head_size) / sum_rows.T[:, :, None]
    grad_rows = lax.dynamic_slice_in_dim(grad_heads, row_start, row_count, 0)
    delta_rows = jnp.sum(grad_rows * attention_rows, axis=2).T
    log_rows = peak_rows + jnp.log(sum_rows)
    log_total, deltas = gather_turned((log_rows, delta_rows), "ctx", (1, 1))
    attn_rows = attention_rows.reshape(row_count, feature_count).astype(jnp.bfloat16)
    probabilities = jnp.exp(scores - log_total[..., None])
    dprobs = jnp.einsum("qhd,khd->hqk", grad_heads, value_heads, preferred_element_type=jnp.float32)
    dscores = (probabilities * (dprobs - deltas[..., None])).astype(jnp.bfloat16)
    prob_rounded = probabilities.astype(jnp.bfloat16)
    query_part = softmax_scale * jnp.einsum(
        "hqk,khd->qhd", dscores, key_heads, preferred_element_type=jnp.float32
    ).reshape(query_count, feature_count)
    query_rows = sum_at_owner(query_part, "ctx", 0).astype(jnp.bfloat16)
    block_shape = (head_count, owner_ways, query_ways, part_rows, slot_count)
    row_shape = (owner_ways, query_ways, part_rows, head_count, head_size)
    key_blocks = softmax_scale * jnp.einsum(
        "hcbrk,cbrhd->bkhd",
        dscores.reshape(block_shape),
        queries.reshape(row_shape),
        preferred_element_type=jnp.float32,
    )
    value_blocks = jnp.einsum(
        "hcbrk,cbrhd->bkhd",
        prob_rounded.reshape(block_shape),
        grad_heads.reshape(row_shape),
        preferred_element_type=jnp.float32,
    )
    key_cols = jnp.sum(key_blocks.astype(jnp.bfloat16).astype(jnp.float32), axis=0).reshape(
        slot_count, feature_count
    )
    value_cols = jnp.sum(value_blocks.astype(jnp.bfloat16).astype(jnp.float32), axis=0).reshape(
        slot_count, feature_count
    )
    attn_final, query_final = (
        lax.all_to_all(attn_rows, "query", split_axis=0, concat_axis=1, tiled=True),
        lax.all_to_all(query_rows, "query", split_axis=0, concat_axis=1, tiled=True),
    )
    return (attn_final, query_final, key_cols.astype(jnp.bfloat16), value_cols.astype(jnp.bfloat16))


def solution(mesh):
    placed = (
        P("query", None),
        P("ctx", "query"),
        P("ctx", "query"),
        P("ctx"),
        P(),
        P("ctx"),
        P("query", None),
    )
    return jax.shard_map(
        local,
        mesh=mesh,
        in_specs=placed,
        out_specs=(
            P(("query", "ctx"), None),
            P(("query", "ctx"), None),
            P("ctx", "query"),
            P("ctx", "query"),
        ),
        check_vma=False,
    )
```

profile of v0, /device:TPU:1, one launch (start us, length us, event | category | flops | bytes accessed | tf_op | source)
XLA Modules:
  0.0 183.3 jit_solution(12638040741019976941)
XLA Ops:
  0.6 1.6 copy.228
  2.3 11.6 %all-to-all-start = ((bf16[32,8,384]{2,0,1:T(8,128)(2,1)}), bf16[32,8,384]{2,0,1:T(8,128)(2,1)S(1)}, u32[]{:S(2)}, u32[]{:S(2)}) async-start(bf16[32,8,384]{2,0,1:T(8,128)(2,1)} %bitcast.82), calls=%async_computation | async-start | bytes 393216 | tf_op jit(solution)/shard_map/all_to_all | solution.py:56
  13.9 2.3 %copy.174 = bf16[1024,384]{0,1:T(8,128)(2,1)} copy(bf16[1024,384]{1,0:T(8,128)(2,1)} %param.8) | data formatting | bytes 1572864 | tf_op args[1]
  16.9 1.2 fusion.17
  18.1 5.7 %all-to-all-done = bf16[32,8,384]{2,0,1:T(8,128)(2,1)S(1)} async-done(((bf16[32,8,384]{2,0,1:T(8,128)(2,1)}), bf16[32,8,384]{2,0,1:T(8,128)(2,1)S(1)}, u32[]{:S(2)}, u32[]{:S(2)}) %all-to-all-start) | async-done | bytes 196640 | tf_op jit(solution)/shard_map/all_to_all | solution.py:56
  24.5 1.9 %fusion.29 = (f32[3,256]{1,0:T(4,128)S(1)}, f32[3,256,1024]{2,1,0:T(8,128)S(1)}) fusion(f32[3,1024]{1,0:T(4,128)S(1)} %fusion.17, bf16[1024,3,128]{0,2,1:T(8,128)(2,1)} %bitcast.91, bf16[256,3,128]{2,1,0:T(4,128)(2,1)S(1)} %reshape_reshape.9, pred[1024]{0:T(1024)(128)(4,1)S(1)} %iota_compare_fusion.2), kind=kOutput, calls=%fused_computation.47 | convolution fusion | flops 204471552 | bytes 4145152 | tf_op jit(solution)/shard_map/qhd,khd->hqk/dot_general | solution.py:93
  27.0 9.1 %all-to-all-start.1 = ((f32[32,3,256]{2,1,0:T(4,128)}), f32[32,3,256]{2,1,0:T(4,128)S(1)}, u32[]{:S(2)}, u32[]{:S(2)}) async-start(f32[32,3,256]{2,1,0:T(4,128)} %broadcast_in_dim.16), calls=%async_computation.1 | async-start | bytes 262144 | tf_op jit(solution)/shard_map/all_to_all | solution.py:10
  36.1 2.3 %copy.177 = bf16[1024,384]{0,1:T(8,128)(2,1)} copy(bf16[1024,384]{1,0:T(8,128)(2,1)} %param.9) | data formatting | bytes 1572864 | tf_op args[2]
  38.4 1.6 copy.227
  40.0 4.8 %all-to-all-done.1 = f32[32,3,256]{2,1,0:T(4,128)S(1)} async-done(((f32[32,3,256]{2,1,0:T(4,128)}), f32[32,3,256]{2,1,0:T(4,128)S(1)}, u32[]{:S(2)}, u32[]{:S(2)}) %all-to-all-start.1) | async-done | bytes 98336 | tf_op jit(solution)/shard_map/all_to_all | solution.py:10
  44.8 3.4 %all-to-all-start.5 = ((bf16[32,8,384]{2,0,1:T(8,128)(2,1)}), bf16[32,8,384]{2,0,1:T(8,128)(2,1)S(1)}, u32[]{:S(2)}, u32[]{:S(2)}) async-start(bf16[32,8,384]{2,0,1:T(8,128)(2,1)} %bitcast.81), calls=%async_computation.5 | async-start | bytes 393216 | tf_op jit(solution)/shard_map/all_to_all | solution.py:57
  48.2 0.9 fusion.1
  49.9 8.3 %all-to-all-done.5 = bf16[32,8,384]{2,0,1:T(8,128)(2,1)S(1)} async-done(((bf16[32,8,384]{2,0,1:T(8,128)(2,1)}), bf16[32,8,384]{2,0,1:T(8,128)(2,1)S(1)}, u32[]{:S(2)}, u32[]{:S(2)}) %all-to-all-start.5) | async-done | bytes 196640 | tf_op jit(solution)/shard_map/all_to_all | solution.py:57
  58.2 6.1 %all-to-all-start.3 = ((f32[32,3,8]{2,1,0:T(4,128)}), f32[32,3,8]{2,1,0:T(4,128)S(1)}, u32[]{:S(2)}, u32[]{:S(2)}) async-start(f32[32,3,8]{2,1,0:T(4,128)} %copy.181), calls=%async_computation.3 | async-start | bytes 131072 | tf_op jit(solution)/shard_map/all_to_all | solution.py:25
  64.4 1.8 fusion.13
  66.2 1.1 copy.180
  67.3 2.0 %reshape_reshape.10 = f32[32,8,384]{2,1,0:T(8,128)} reshape(f32[256,3,128]{2,1,0:T(4,128)} %copy.180) | data formatting | bytes 786432 | tf_op jit(solution)/shard_map/reshape;reshape | solution.py:19
  69.3 2.9 %all-to-all-done.3 = f32[32,3,8]{2,1,0:T(4,128)S(1)} async-done(((f32[32,3,8]{2,1,0:T(4,128)}), f32[32,3,8]{2,1,0:T(4,128)S(1)}, u32[]{:S(2)}, u32[]{:S(2)}) %all-to-all-start.3) | async-done | bytes 3104 | tf_op jit(solution)/shard_map/all_to_all | solution.py:25
  72.8 4.8 %all-to-all-start.2 = ((f32[32,8,384]{2,1,0:T(8,128)}), f32[32,8,384]{2,1,0:T(8,128)S(1)}, u32[]{:S(2)}, u32[]{:S(2)}) async-start(f32[32,8,384]{2,1,0:T(8,128)} %reshape_reshape.10), calls=%async_computation.2 | async-start | bytes 786432 | tf_op jit(solution)/shard_map/all_to_all | solution.py:25
  77.6 1.7 copy.229
  79.3 1.7 reshape_reshape.11
  80.9 1.7 copy.185
  82.6 0.9 reduce_sum.78
  84.1 7.5 %all-to-all-done.2 = f32[32,8,384]{2,1,0:T(8,128)S(1)} async-done(((f32[32,8,384]{2,1,0:T(8,128)}), f32[32,8,384]{2,1,0:T(8,128)S(1)}, u32[]{:S(2)}, u32[]{:S(2)}) %all-to-all-start.2) | async-done | bytes 393248 | tf_op jit(solution)/shard_map/all_to_all | solution.py:25
  91.7 0.9 fusion.24
  92.5 0.7 pad_maximum_fusion
  93.3 39.9 %all_gather.3 = f32[256,6]{1,0:T(8,128)S(1)} all-gather(f32[8,6]{1,0:T(8,128)S(1)} %copy.186), channel_id=1, replica_groups=mesh['query'=8,'ctx'=32] {'ctx'}, dimensions={0}, use_global_device_ids=true | all-gather | bytes 6336 | tf_op jit(solution)/shard_map/all_gather | solution.py:33
  133.4 2.1 %multiply_convert_fusion.1 = bf16[3,256,1024]{2,1,0:T(8,128)(2,1)S(1)} fusion(f32[3,256,1024]{2,1,0:T(8,128)S(1)} %get-tuple-element.41, bf16[256,3,128]{2,0,1:T(8,128)(2,1)} %copy.185, bf16[1024,3,128]{0,2,1:T(8,128)(2,1)} %bitcast.87, f32[3,256]{1,0:T(4,128)S(1)} %copy.190, f32[3,256]{1,0:T(4,128)S(1)} %copy.187), kind=kOutput, calls=%fused_computation.3 | convolution fusion | flops 204472320 | bytes 5707776 | tf_op jit(solution)/shard_map/qhd,khd->hqk/dot_general | solution.py:122
  135.6 1.1 copy-done.1
  137.3 1.1 copy.192
  138.4 2.0 %mul.66 = f32[32,8,384]{2,1,0:T(8,128)} reshape(f32[256,3,128]{2,1,0:T(4,128)} %copy.192) | data formatting | bytes 786432 | tf_op jit(solution)/shard_map/mul | solution.py:125
  140.4 3.8 %all-to-all-start.6 = ((f32[32,8,384]{2,1,0:T(8,128)}), f32[32,8,384]{2,1,0:T(8,128)S(1)}, u32[]{:S(2)}, u32[]{:S(2)}) async-start(f32[32,8,384]{2,1,0:T(8,128)} %mul.66), calls=%async_computation.6 | async-start | bytes 786432 | tf_op jit(solution)/shard_map/all_to_all | solution.py:25
  144.3 1.3 fusion.23
  146.1 1.3 reduce.4
  147.5 0.7 reshape.124
  148.2 6.0 %fusion = bf16[3,1024,128]{2,1,0:T(8,128)(2,1)} fusion(bf16[3,32,8,1024]{3,2,1,0:T(8,128)(2,1)} %bitcast.88, bf16[32,8,3,128]{3,1,2,0:T(8,128)(2,1)} %bitcast.94), kind=kOutput, calls=%fused_computation.1 | convolution fusion | flops 210370560 | bytes 2555904 | tf_op jit(solution)/shard_map/hcbrk,cbrhd->bkhd/dot_general | solution.py:131
  154.2 4.0 %all-to-all-done.6 = f32[32,8,384]{2,1,0:T(8,128)S(1)} async-done(((f32[32,8,384]{2,1,0:T(8,128)}), f32[32,8,384]{2,1,0:T(8,128)S(1)}, u32[]{:S(2)}, u32[]{:S(2)}) %all-to-all-start.6) | async-done | bytes 393248 | tf_op jit(solution)/shard_map/all_to_all | solution.py:25
  158.2 3.3 %all-to-all-start.4 = ((bf16[8,2,192]{2,1,0:T(2,128)(2,1)}), bf16[8,2,192]{2,1,0:T(2,128)(2,1)S(1)}, u32[]{:S(2)}, u32[]{:S(2)}) async-start(bf16[8,2,192]{2,1,0:T(2,128)(2,1)} %reshape.124), calls=%async_computation.4 | async-start | bytes 16384 | tf_op jit(solution)/shard_map/all_to_all | solution.py:150
  161.6 1.6 fusion.4
  163.3 0.7 reduce.5
  164.7 5.8 %all-to-all-done.4 = bf16[8,2,192]{2,1,0:T(2,128)(2,1)S(1)} async-done(((bf16[8,2,192]{2,1,0:T(2,128)(2,1)}), bf16[8,2,192]{2,1,0:T(2,128)(2,1)S(1)}, u32[]{:S(2)}, u32[]{:S(2)}) %all-to-all-start.4) | async-done | bytes 6176 | tf_op jit(solution)/shard_map/all_to_all | solution.py:150
  170.5 3.3 %all-to-all-start.7 = ((bf16[8,2,192]{2,1,0:T(2,128)(2,1)}), bf16[8,2,192]{2,1,0:T(2,128)(2,1)S(1)}, u32[]{:S(2)}, u32[]{:S(2)}) async-start(bf16[8,2,192]{2,1,0:T(2,128)(2,1)} %reshape.126), calls=%async_computation.7 | async-start | bytes 16384 | tf_op jit(solution)/shard_map/all_to_all | solution.py:151
  173.8 4.2 %convert_reduce_fusion = bf16[3,1024,128]{2,1,0:T(8,128)(2,1)S(1)} fusion(bf16[3,32,8,1024]{3,2,1,0:T(8,128)(2,1)} %fusion.4, bf16[32,8,3,128]{3,1,2,0:T(8,128)(2,1)} %bitcast.96), kind=kOutput, calls=%fused_computation.2 | convolution fusion | flops 207224832 | bytes 2555904 | tf_op jit(solution)/shard_map/hcbrk,cbrhd->bkhd/dot_general | solution.py:137
  178.3 1.2 copy.200
  179.7 1.2 copy.201
  180.9 0.7 reshape.125
  181.6 1.1 all-to-all-done.7
  182.7 0.7 reshape.127
  (39 shorter events, 6.3 us)
Async XLA Ops:
  0.6 16.2 %copy-start = (f32[5,24]{1,0:T(8,128)S(1)}, f32[5,24]{1,0:T(8,128)}, u32[]{:S(2)}) copy-start(f32[5,24]{1,0:T(8,128)} %param.11) | copy-start | bytes 1444
  2.3 21.5 %all-to-all-start = ((bf16[32,8,384]{2,0,1:T(8,128)(2,1)}), bf16[32,8,384]{2,0,1:T(8,128)(2,1)S(1)}, u32[]{:S(2)}, u32[]{:S(2)}) async-start(bf16[32,8,384]{2,0,1:T(8,128)(2,1)} %bitcast.82), calls=%async_computation | async-start | bytes 393216 | tf_op jit(solution)/shard_map/all_to_all | solution.py:56
  23.8 0.7 copy-start.3
  27.0 17.8 %all-to-all-start.1 = ((f32[32,3,256]{2,1,0:T(4,128)}), f32[32,3,256]{2,1,0:T(4,128)S(1)}, u32[]{:S(2)}, u32[]{:S(2)}) async-start(f32[32,3,256]{2,1,0:T(4,128)} %broadcast_in_dim.16), calls=%async_computation.1 | async-start | bytes 262144 | tf_op jit(solution)/shard_map/all_to_all | solution.py:10
  44.8 13.4 %all-to-all-start.5 = ((bf16[32,8,384]{2,0,1:T(8,128)(2,1)}), bf16[32,8,384]{2,0,1:T(8,128)(2,1)S(1)}, u32[]{:S(2)}, u32[]{:S(2)}) async-start(bf16[32,8,384]{2,0,1:T(8,128)(2,1)} %bitcast.81), calls=%async_computation.5 | async-start | bytes 393216 | tf_op jit(solution)/shard_map/all_to_all | solution.py:57
  58.2 11.0 %copy-start.5 = (bf16[32,8,384]{2,0,1:T(8,128)(2,1)}, bf16[32,8,384]{2,0,1:T(8,128)(2,1)S(1)}, u32[]{:S(2)}) copy-start(bf16[32,8,384]{2,0,1:T(8,128)(2,1)S(1)} %all-to-all-done.5) | copy-start | bytes 589828
  58.2 13.9 %all-to-all-start.3 = ((f32[32,3,8]{2,1,0:T(4,128)}), f32[32,3,8]{2,1,0:T(4,128)S(1)}, u32[]{:S(2)}, u32[]{:S(2)}) async-start(f32[32,3,8]{2,1,0:T(4,128)} %copy.181), calls=%async_computation.3 | async-start | bytes 131072 | tf_op jit(solution)/shard_map/all_to_all | solution.py:25
  72.2 0.6 copy-start.6
  72.8 18.8 %all-to-all-start.2 = ((f32[32,8,384]{2,1,0:T(8,128)}), f32[32,8,384]{2,1,0:T(8,128)S(1)}, u32[]{:S(2)}, u32[]{:S(2)}) async-start(f32[32,8,384]{2,1,0:T(8,128)} %reshape_reshape.10), calls=%async_computation.2 | async-start | bytes 786432 | tf_op jit(solution)/shard_map/all_to_all | solution.py:25
  83.5 0.7 copy-start.9
  133.4 3.9 %copy-start.7 = (f32[3,256]{1,0:T(4,128)}, f32[3,256]{1,0:T(4,128)S(1)}, u32[]{:S(2)}) copy-start(f32[3,256]{1,0:T(4,128)S(1)} %copy.187) | copy-start | bytes 9220
  133.4 3.3 %copy-start.2 = (bf16[1024,384]{0,1:T(8,128)(2,1)S(1)}, bf16[1024,384]{0,1:T(8,128)(2,1)}, u32[]{:S(2)}) copy-start(bf16[1024,384]{0,1:T(8,128)(2,1)} %copy.174) | copy-start | bytes 2359300
  135.6 1.2 copy-start.1
  140.4 17.8 %all-to-all-start.6 = ((f32[32,8,384]{2,1,0:T(8,128)}), f32[32,8,384]{2,1,0:T(8,128)S(1)}, u32[]{:S(2)}, u32[]{:S(2)}) async-start(f32[32,8,384]{2,1,0:T(8,128)} %mul.66), calls=%async_computation.6 | async-start | bytes 786432 | tf_op jit(solution)/shard_map/all_to_all | solution.py:25
  148.2 13.4 %copy-start.8 = (f32[3,256]{1,0:T(4,128)S(1)}, f32[3,256]{1,0:T(4,128)}, u32[]{:S(2)}) copy-start(f32[3,256]{1,0:T(4,128)} %copy-done.7) | copy-start | bytes 9220
  158.2 12.2 %all-to-all-start.4 = ((bf16[8,2,192]{2,1,0:T(2,128)(2,1)}), bf16[8,2,192]{2,1,0:T(2,128)(2,1)S(1)}, u32[]{:S(2)}, u32[]{:S(2)}) async-start(bf16[8,2,192]{2,1,0:T(2,128)(2,1)} %reshape.124), calls=%async_computation.4 | async-start | bytes 16384 | tf_op jit(solution)/shard_map/all_to_all | solution.py:150
  163.2 14.7 %copy-start.4 = (bf16[3,1024,128]{2,1,0:T(8,128)(2,1)S(1)}, bf16[3,1024,128]{2,1,0:T(8,128)(2,1)}, u32[]{:S(2)}) copy-start(bf16[3,1024,128]{2,1,0:T(8,128)(2,1)} %fusion) | copy-start | bytes 2359300
  170.5 12.2 %all-to-all-start.7 = ((bf16[8,2,192]{2,1,0:T(2,128)(2,1)}), bf16[8,2,192]{2,1,0:T(2,128)(2,1)S(1)}, u32[]{:S(2)}, u32[]{:S(2)}) async-start(bf16[8,2,192]{2,1,0:T(2,128)(2,1)} %reshape.126), calls=%async_computation.7 | async-start | bytes 16384 | tf_op jit(solution)/shard_map/all_to_all | solution.py:151
where the time goes:
time: 185 us; the launch traced here: 183 us
  starting transfers between devices  45.6 us (25%)
  waiting for transfers between devices  40 us (22%)
  blocking collectives  39.9 us (22%)
  local copies, waits for them, and re-layouts  29.4 us (16%)
  matrix products  17.8 us (10%)
  other arithmetic  9.17 us (5%)
    all_gather x1, blocking collectives, gather_turned(): out = lax.all_gather(both, axis, axis=0, tiled=True)  39.9 us
    all_to_all x3, starting transfers between devices, sum_at_owner(): pieces = lax.all_to_all(split_up(x, dim, peers), axis, 0, 0, tiled=True)  14.8 us
    all_to_all x3, waiting for transfers between devices, sum_at_owner(): pieces = lax.all_to_all(split_up(x, dim, peers), axis, 0, 0, tiled=True)  14.4 us
    unnamed x28, local copies, waits for them, and re-layouts  12 us
    all_to_all x1, starting transfers between devices, local(): lax.all_to_all(query_states, 'query', split_axis=1, concat_axis=0, tiled=...  11.6 us
    all_to_all x1, starting transfers between devices, copy_for_each(): return lax.all_to_all(copies, axis, split_axis=0, concat_axis=0, tiled=True)  9.11 us
    all_to_all x1, waiting for transfers between devices, local(): lax.all_to_all(out_grad, 'query', split_axis=1, concat_axis=0, tiled=True)  8.29 us
    dot_general x1, matrix products, local(): jnp.einsum('hcbrk,cbrhd->bkhd', dscores.reshape(block_shape), queries.res...  6.05 us
  transfers between devices with their start and end apart: 8, of which 8 were waited for; matrix products, arithmetic and copies ran while one was open for 23% of the time, Pallas kernels for 0%

commit v1 on v0

--- a/solution.py
+++ b/solution.py
@@ -30,7 +30,10 @@
     turned = [jnp.moveaxis(a, dim, 0) for a, dim in zip(arrays, dims)]
     widths = [t[0].size for t in turned]
     both = jnp.concatenate([t.reshape(-1, w) for t, w in zip(turned, widths)], axis=1)
-    out = lax.all_gather(both, axis, axis=0, tiled=True)
+    devices = lax.axis_size(axis)
+    blocks = jnp.stack([both for _ in range(devices)])
+    blocks = lax.all_to_all(blocks, axis, split_axis=0, concat_axis=0)
+    out = jnp.concatenate(blocks, axis=0)
     pieces = jnp.split(out, [sum(widths[:k]) for k in range(1, len(widths))], axis=1)
     return tuple(
         (

time: 185 us -> 156 us (0.84)
  blocking collectives: 39.9 us -> 0 us
  starting transfers between devices: 45.6 us -> 53.5 us
  waiting for transfers between devices: 40 us -> 46.7 us
  matrix products: 17.8 us -> 15.7 us
    all_gather x1 -> x0, blocking collectives: 39.9 us -> none  [gather_turned(): out = lax.all_gather(both, axis, axis=0, tiled=True)]
    all_to_all x0 -> x1, waiting for transfers between devices: none -> 6.17 us  [gather_turned(): blocks = lax.all_to_all(blocks, axis, split_axis=0, concat_axis=0)]
    all_to_all x1, waiting for transfers between devices: 5.79 us -> 1.77 us  [local(): lax.all_to_all(attn_rows, 'query', split_axis=0, concat_axis=1, tiled=True)]
    all_to_all x3, waiting for transfers between devices: 14.4 us -> 18 us  [sum_at_owner(): pieces = lax.all_to_all(split_up(x, dim, peers), axis, 0, 0, tiled=True)]
    all_to_all x0 -> x1, starting transfers between devices: none -> 3.64 us  [gather_turned(): blocks = lax.all_to_all(blocks, axis, split_axis=0, concat_axis=0)]
    all_to_all x1, starting transfers between devices: 3.32 us -> 6.33 us  [local(): lax.all_to_all(query_rows, 'query', split_axis=0, concat_axis=1, tiled=True)]
    dot_general x1, matrix products: 6.05 us -> 4.07 us  [local(): jnp.einsum('hcbrk,cbrhd->bkhd', dscores.reshape(block_shape), queries.res...]
    unnamed x28 -> x32, local copies, waits for them, and re-layouts: 12 us -> 12.1 us
  transfers between devices with their start and end apart: 8 -> 9, of which waited for: 8 -> 9; matrix products, arithmetic and copies ran while one was open for 23% -> 27% of each run, Pallas kernels for 0% -> 0%
where the time goes in v1:
time: 156 us; the launch traced here: 155 us
  starting transfers between devices  53.5 us (34%)
  waiting for transfers between devices  46.7 us (30%)
  local copies, waits for them, and re-layouts  29.9 us (19%)
  matrix products  15.7 us (10%)
  other arithmetic  7.69 us (5%)
    all_to_all x3, waiting for transfers between devices, sum_at_owner(): pieces = lax.all_to_all(split_up(x, dim, peers), axis, 0, 0, tiled=True)  18 us
    all_to_all x3, starting transfers between devices, sum_at_owner(): pieces = lax.all_to_all(split_up(x, dim, peers), axis, 0, 0, tiled=True)  16 us
    unnamed x32, local copies, waits for them, and re-layouts  12.1 us
    all_to_all x1, starting transfers between devices, local(): lax.all_to_all(query_states, 'query', split_axis=1, concat_axis=0, tiled=...  11.6 us
    all_to_all x1, starting transfers between devices, copy_for_each(): return lax.all_to_all(copies, axis, split_axis=0, concat_axis=0, tiled=True)  9.11 us
    all_to_all x1, waiting for transfers between devices, local(): lax.all_to_all(out_grad, 'query', split_axis=1, concat_axis=0, tiled=True)  8.29 us
    all_to_all x1, starting transfers between devices, local(): lax.all_to_all(query_rows, 'query', split_axis=0, concat_axis=1, tiled=True)  6.33 us
    all_to_all x1, waiting for transfers between devices, gather_turned(): blocks = lax.all_to_all(blocks, axis, split_axis=0, concat_axis=0)  6.17 us
  transfers between devices with their start and end apart: 9, of which 9 were waited for; matrix products, arithmetic and copies ran while one was open for 27% of the time, Pallas kernels for 0%

profile of v1, /device:TPU:1, one launch (start us, length us, event | category | flops | bytes accessed | tf_op | source)
XLA Modules:
  0.0 155.0 jit_solution(530626293258355828)
XLA Ops:
  0.6 1.6 %copy.183 = bf16[4,8,8,384]{3,2,0,1:T(8,128)(2,1)} copy(bf16[4,8,8,384]{3,2,1,0:T(8,128)(2,1)} %bitcast.101) | data formatting | bytes 393216 | tf_op jit(solution)/shard_map/all_to_all | solution.py:59
  2.3 11.6 %all-to-all-start = ((bf16[32,8,384]{2,0,1:T(8,128)(2,1)}), bf16[32,8,384]{2,0,1:T(8,128)(2,1)S(1)}, u32[]{:S(2)}, u32[]{:S(2)}) async-start(bf16[32,8,384]{2,0,1:T(8,128)(2,1)} %bitcast.84), calls=%async_computation | async-start | bytes 393216 | tf_op jit(solution)/shard_map/all_to_all | solution.py:59
  13.9 2.3 %copy.131 = bf16[1024,384]{0,1:T(8,128)(2,1)} copy(bf16[1024,384]{1,0:T(8,128)(2,1)} %param.8) | data formatting | bytes 1572864 | tf_op args[1]
  16.9 1.2 fusion.17
  18.1 5.7 %all-to-all-done = bf16[32,8,384]{2,0,1:T(8,128)(2,1)S(1)} async-done(((bf16[32,8,384]{2,0,1:T(8,128)(2,1)}), bf16[32,8,384]{2,0,1:T(8,128)(2,1)S(1)}, u32[]{:S(2)}, u32[]{:S(2)}) %all-to-all-start) | async-done | bytes 196640 | tf_op jit(solution)/shard_map/all_to_all | solution.py:59
  24.5 1.9 %fusion.29 = (f32[3,256]{1,0:T(4,128)S(1)}, f32[3,256,1024]{2,1,0:T(8,128)S(1)}) fusion(f32[3,1024]{1,0:T(4,128)S(1)} %fusion.17, bf16[1024,3,128]{0,2,1:T(8,128)(2,1)} %bitcast.93, bf16[256,3,128]{2,1,0:T(4,128)(2,1)S(1)} %reshape_reshape.9, pred[1024]{0:T(1024)(128)(4,1)S(1)} %iota_compare_fusion.2), kind=kOutput, calls=%fused_computation.47 | convolution fusion | flops 204471552 | bytes 4145152 | tf_op jit(solution)/shard_map/qhd,khd->hqk/dot_general | solution.py:96
  27.1 9.1 %all-to-all-start.1 = ((f32[32,3,256]{2,1,0:T(4,128)}), f32[32,3,256]{2,1,0:T(4,128)S(1)}, u32[]{:S(2)}, u32[]{:S(2)}) async-start(f32[32,3,256]{2,1,0:T(4,128)} %broadcast_in_dim.16), calls=%async_computation.1 | async-start | bytes 262144 | tf_op jit(solution)/shard_map/all_to_all | solution.py:10
  36.2 2.3 %copy.134 = bf16[1024,384]{0,1:T(8,128)(2,1)} copy(bf16[1024,384]{1,0:T(8,128)(2,1)} %param.9) | data formatting | bytes 1572864 | tf_op args[2]
  38.5 1.6 %copy.182 = bf16[4,8,8,384]{3,2,0,1:T(8,128)(2,1)} copy(bf16[4,8,8,384]{3,2,1,0:T(8,128)(2,1)} %bitcast.102) | data formatting | bytes 393216 | tf_op jit(solution)/shard_map/all_to_all | solution.py:60
  40.1 4.8 %all-to-all-done.1 = f32[32,3,256]{2,1,0:T(4,128)S(1)} async-done(((f32[32,3,256]{2,1,0:T(4,128)}), f32[32,3,256]{2,1,0:T(4,128)S(1)}, u32[]{:S(2)}, u32[]{:S(2)}) %all-to-all-start.1) | async-done | bytes 98336 | tf_op jit(solution)/shard_map/all_to_all | solution.py:10
  44.9 3.4 %all-to-all-start.5 = ((bf16[32,8,384]{2,0,1:T(8,128)(2,1)}), bf16[32,8,384]{2,0,1:T(8,128)(2,1)S(1)}, u32[]{:S(2)}, u32[]{:S(2)}) async-start(bf16[32,8,384]{2,0,1:T(8,128)(2,1)} %bitcast.83), calls=%async_computation.5 | async-start | bytes 393216 | tf_op jit(solution)/shard_map/all_to_all | solution.py:60
  48.3 0.9 fusion.1
  50.0 8.3 %all-to-all-done.5 = bf16[32,8,384]{2,0,1:T(8,128)(2,1)S(1)} async-done(((bf16[32,8,384]{2,0,1:T(8,128)(2,1)}), bf16[32,8,384]{2,0,1:T(8,128)(2,1)S(1)}, u32[]{:S(2)}, u32[]{:S(2)}) %all-to-all-start.5) | async-done | bytes 196640 | tf_op jit(solution)/shard_map/all_to_all | solution.py:60
  58.3 6.1 %all-to-all-start.3 = ((f32[32,3,8]{2,1,0:T(4,128)}), f32[32,3,8]{2,1,0:T(4,128)S(1)}, u32[]{:S(2)}, u32[]{:S(2)}) async-start(f32[32,3,8]{2,1,0:T(4,128)} %copy.138), calls=%async_computation.3 | async-start | bytes 131072 | tf_op jit(solution)/shard_map/all_to_all | solution.py:25
  64.4 1.8 %fusion.13 = f32[256,3,128]{2,0,1:T(8,128)S(1)} fusion(bf16[1024,3,128]{0,2,1:T(8,128)(2,1)} %bitcast.88, f32[3,256,1024]{2,1,0:T(8,128)S(1)} %get-tuple-element.37, f32[3,256]{1,0:T(4,128)S(1)} %get-tuple-element.36, f32[256,3]{0,1:T(4,128)S(1)} %get-tuple-element.35), kind=kOutput, calls=%fused_computation.16 | convolution fusion | flops 202997760 | bytes 4331520 | tf_op jit(solution)/shard_map/hqk,khd->qhd/dot_general | solution.py:103
  66.3 1.1 copy.137
  67.3 2.0 %reshape_reshape.10 = f32[32,8,384]{2,1,0:T(8,128)} reshape(f32[256,3,128]{2,1,0:T(4,128)} %copy.137) | data formatting | bytes 786432 | tf_op jit(solution)/shard_map/reshape;reshape | solution.py:19
  69.3 2.9 %all-to-all-done.3 = f32[32,3,8]{2,1,0:T(4,128)S(1)} async-done(((f32[32,3,8]{2,1,0:T(4,128)}), f32[32,3,8]{2,1,0:T(4,128)S(1)}, u32[]{:S(2)}, u32[]{:S(2)}) %all-to-all-start.3) | async-done | bytes 3104 | tf_op jit(solution)/shard_map/all_to_all | solution.py:25
  72.8 4.8 %all-to-all-start.2 = ((f32[32,8,384]{2,1,0:T(8,128)}), f32[32,8,384]{2,1,0:T(8,128)S(1)}, u32[]{:S(2)}, u32[]{:S(2)}) async-start(f32[32,8,384]{2,1,0:T(8,128)} %reshape_reshape.10), calls=%async_computation.2 | async-start | bytes 786432 | tf_op jit(solution)/shard_map/all_to_all | solution.py:25
  77.7 1.7 %copy.184 = bf16[32,8,384]{2,1,0:T(8,128)(2,1)} copy(bf16[32,8,384]{2,0,1:T(8,128)(2,1)} %copy-done.9) | data formatting | bytes 393216 | tf_op jit(solution)/shard_map/all_to_all | solution.py:60
  79.3 1.7 %reshape_reshape.11 = bf16[256,3,128]{2,1,0:T(4,128)(2,1)} reshape(bf16[32,8,1,384]{3,1,0,2:T(8,128)(2,1)} %bitcast.97) | data formatting | bytes 393216 | tf_op jit(solution)/shard_map/reshape;reshape | solution.py:84
  81.0 1.7 %copy.142 = bf16[256,3,128]{2,0,1:T(8,128)(2,1)} copy(bf16[256,3,128]{2,1,0:T(4,128)(2,1)} %reshape_reshape.11) | data formatting | bytes 393216 | tf_op jit(solution)/shard_map/reshape;reshape | solution.py:84
  82.7 0.9 reduce_sum.78
  84.2 7.5 %all-to-all-done.2 = f32[32,8,384]{2,1,0:T(8,128)S(1)} async-done(((f32[32,8,384]{2,1,0:T(8,128)}), f32[32,8,384]{2,1,0:T(8,128)S(1)}, u32[]{:S(2)}, u32[]{:S(2)}) %all-to-all-start.2) | async-done | bytes 393248 | tf_op jit(solution)/shard_map/all_to_all | solution.py:25
  91.7 0.9 fusion.24
  92.6 0.7 pad_maximum_fusion
  93.9 3.6 %all-to-all-start.6 = ((f32[32,8,6]{1,2,0:T(8,128)}), f32[32,8,6]{1,2,0:T(8,128)S(1)}, u32[]{:S(2)}, u32[]{:S(2)}) async-start(f32[32,8,6]{1,2,0:T(8,128)} %stack.2), calls=%async_computation.6 | async-start | bytes 262144 | tf_op jit(solution)/shard_map/all_to_all | solution.py:35
  97.6 0.8 fusion.23
  99.4 0.7 reshape.130
  100.1 6.2 %all-to-all-done.6 = f32[32,8,6]{1,2,0:T(8,128)S(1)} async-done(((f32[32,8,6]{1,2,0:T(8,128)}), f32[32,8,6]{1,2,0:T(8,128)S(1)}, u32[]{:S(2)}, u32[]{:S(2)}) %all-to-all-start.6) | async-done | bytes 6176 | tf_op jit(solution)/shard_map/all_to_all | solution.py:35
  106.3 3.3 %all-to-all-start.4 = ((bf16[8,2,192]{2,1,0:T(2,128)(2,1)}), bf16[8,2,192]{2,1,0:T(2,128)(2,1)S(1)}, u32[]{:S(2)}, u32[]{:S(2)}) async-start(bf16[8,2,192]{2,1,0:T(2,128)(2,1)} %reshape.130), calls=%async_computation.4 | async-start | bytes 16384 | tf_op jit(solution)/shard_map/all_to_all | solution.py:153
  109.8 2.1 %multiply_convert_fusion.1 = bf16[3,256,1024]{2,1,0:T(8,128)(2,1)S(1)} fusion(f32[3,256,1024]{2,1,0:T(8,128)S(1)} %get-tuple-element.37, bf16[256,3,128]{2,0,1:T(8,128)(2,1)} %copy.142, bf16[1024,3,128]{0,2,1:T(8,128)(2,1)} %bitcast.89, f32[3,256]{1,0:T(4,128)S(1)} %get-tuple-element.33, f32[3,256]{1,0:T(4,128)S(1)} %get-tuple-element.32), kind=kOutput, calls=%fused_computation.3 | convolution fusion | flops 204472320 | bytes 5707776 | tf_op jit(solution)/shard_map/qhd,khd->hqk/dot_general | solution.py:125
  111.9 1.1 copy-done.1
  113.6 1.1 copy.147
  114.7 2.0 %mul.66 = f32[32,8,384]{2,1,0:T(8,128)} reshape(f32[256,3,128]{2,1,0:T(4,128)} %copy.147) | data formatting | bytes 786432 | tf_op jit(solution)/shard_map/mul | solution.py:128
  116.7 1.8 %all-to-all-done.4 = bf16[8,2,192]{2,1,0:T(2,128)(2,1)S(1)} async-done(((bf16[8,2,192]{2,1,0:T(2,128)(2,1)}), bf16[8,2,192]{2,1,0:T(2,128)(2,1)S(1)}, u32[]{:S(2)}, u32[]{:S(2)}) %all-to-all-start.4) | async-done | bytes 6176 | tf_op jit(solution)/shard_map/all_to_all | solution.py:153
  118.5 5.1 %all-to-all-start.7 = ((f32[32,8,384]{2,1,0:T(8,128)}), f32[32,8,384]{2,1,0:T(8,128)S(1)}, u32[]{:S(2)}, u32[]{:S(2)}) async-start(f32[32,8,384]{2,1,0:T(8,128)} %mul.66), calls=%async_computation.7 | async-start | bytes 786432 | tf_op jit(solution)/shard_map/all_to_all | solution.py:25
  123.6 0.7 reshape.131
  124.3 1.6 %fusion.4 = bf16[3,32,8,1024]{3,2,1,0:T(8,128)(2,1)} fusion(f32[3,256,1024]{2,1,0:T(8,128)S(1)} %get-tuple-element.37, f32[3,256]{1,0:T(4,128)S(1)} %get-tuple-element.32), kind=kLoop, calls=%fused_computation.10 | loop fusion | flops 1572864 | bytes 4721664 | tf_op jit(solution)/shard_map/reshape.10
  125.9 4.1 %fusion = bf16[3,1024,128]{2,1,0:T(8,128)(2,1)S(1)} fusion(bf16[3,32,8,1024]{3,2,1,0:T(8,128)(2,1)S(1)} %bitcast.90, bf16[32,8,3,128]{3,1,2,0:T(8,128)(2,1)S(1)} %bitcast.96), kind=kOutput, calls=%fused_computation.1 | convolution fusion | flops 210370560 | bytes 2555904 | tf_op jit(solution)/shard_map/hcbrk,cbrhd->bkhd/dot_general | solution.py:134
  130.0 7.7 %all-to-all-done.7 = f32[32,8,384]{2,1,0:T(8,128)S(1)} async-done(((f32[32,8,384]{2,1,0:T(8,128)}), f32[32,8,384]{2,1,0:T(8,128)S(1)}, u32[]{:S(2)}, u32[]{:S(2)}) %all-to-all-start.7) | async-done | bytes 393248 | tf_op jit(solution)/shard_map/all_to_all | solution.py:25
  138.3 0.7 reshape.132
  139.0 6.3 %all-to-all-start.8 = ((bf16[8,2,192]{2,1,0:T(2,128)(2,1)}), bf16[8,2,192]{2,1,0:T(2,128)(2,1)S(1)}, u32[]{:S(2)}, u32[]{:S(2)}) async-start(bf16[8,2,192]{2,1,0:T(2,128)(2,1)} %reshape.132), calls=%async_computation.8 | async-start | bytes 16384 | tf_op jit(solution)/shard_map/all_to_all | solution.py:154
  145.3 4.0 %convert_reduce_fusion = bf16[3,1024,128]{2,1,0:T(8,128)(2,1)} fusion(bf16[3,32,8,1024]{3,2,1,0:T(8,128)(2,1)S(1)} %copy-done.4, bf16[32,8,3,128]{3,1,2,0:T(8,128)(2,1)S(1)} %bitcast.98), kind=kOutput, calls=%fused_computation.2 | convolution fusion | flops 207224832 | bytes 2555904 | tf_op jit(solution)/shard_map/hcbrk,cbrhd->bkhd/dot_general | solution.py:140
  149.7 1.2 copy.155
  151.1 1.2 copy.156
  152.3 2.0 %all-to-all-done.8 = bf16[8,2,192]{2,1,0:T(2,128)(2,1)S(1)} async-done(((bf16[8,2,192]{2,1,0:T(2,128)(2,1)}), bf16[8,2,192]{2,1,0:T(2,128)(2,1)S(1)}, u32[]{:S(2)}, u32[]{:S(2)}) %all-to-all-start.8) | async-done | bytes 6176 | tf_op jit(solution)/shard_map/all_to_all | solution.py:154
  154.3 0.7 reshape.133
  (44 shorter events, 7.2 us)
Async XLA Ops:
  0.6 16.2 %copy-start = (f32[5,24]{1,0:T(8,128)S(1)}, f32[5,24]{1,0:T(8,128)}, u32[]{:S(2)}) copy-start(f32[5,24]{1,0:T(8,128)} %param.11) | copy-start | bytes 1444
  2.3 21.5 %all-to-all-start = ((bf16[32,8,384]{2,0,1:T(8,128)(2,1)}), bf16[32,8,384]{2,0,1:T(8,128)(2,1)S(1)}, u32[]{:S(2)}, u32[]{:S(2)}) async-start(bf16[32,8,384]{2,0,1:T(8,128)(2,1)} %bitcast.84), calls=%async_computation | async-start | bytes 393216 | tf_op jit(solution)/shard_map/all_to_all | solution.py:59
  23.8 0.7 copy-start.5
  27.1 17.8 %all-to-all-start.1 = ((f32[32,3,256]{2,1,0:T(4,128)}), f32[32,3,256]{2,1,0:T(4,128)S(1)}, u32[]{:S(2)}, u32[]{:S(2)}) async-start(f32[32,3,256]{2,1,0:T(4,128)} %broadcast_in_dim.16), calls=%async_computation.1 | async-start | bytes 262144 | tf_op jit(solution)/shard_map/all_to_all | solution.py:10
  44.9 13.4 %all-to-all-start.5 = ((bf16[32,8,384]{2,0,1:T(8,128)(2,1)}), bf16[32,8,384]{2,0,1:T(8,128)(2,1)S(1)}, u32[]{:S(2)}, u32[]{:S(2)}) async-start(bf16[32,8,384]{2,0,1:T(8,128)(2,1)} %bitcast.83), calls=%async_computation.5 | async-start | bytes 393216 | tf_op jit(solution)/shard_map/all_to_all | solution.py:60
  58.3 11.0 %copy-start.9 = (bf16[32,8,384]{2,0,1:T(8,128)(2,1)}, bf16[32,8,384]{2,0,1:T(8,128)(2,1)S(1)}, u32[]{:S(2)}) copy-start(bf16[32,8,384]{2,0,1:T(8,128)(2,1)S(1)} %all-to-all-done.5) | copy-start | bytes 589828
  58.3 13.9 %all-to-all-start.3 = ((f32[32,3,8]{2,1,0:T(4,128)}), f32[32,3,8]{2,1,0:T(4,128)S(1)}, u32[]{:S(2)}, u32[]{:S(2)}) async-start(f32[32,3,8]{2,1,0:T(4,128)} %copy.138), calls=%async_computation.3 | async-start | bytes 131072 | tf_op jit(solution)/shard_map/all_to_all | solution.py:25
  72.2 0.6 copy-start.10
  72.8 18.8 %all-to-all-start.2 = ((f32[32,8,384]{2,1,0:T(8,128)}), f32[32,8,384]{2,1,0:T(8,128)S(1)}, u32[]{:S(2)}, u32[]{:S(2)}) async-start(f32[32,8,384]{2,1,0:T(8,128)} %reshape_reshape.10), calls=%async_computation.2 | async-start | bytes 786432 | tf_op jit(solution)/shard_map/all_to_all | solution.py:25
  83.6 0.7 copy-start.11
  93.9 12.3 %all-to-all-start.6 = ((f32[32,8,6]{1,2,0:T(8,128)}), f32[32,8,6]{1,2,0:T(8,128)S(1)}, u32[]{:S(2)}, u32[]{:S(2)}) async-start(f32[32,8,6]{1,2,0:T(8,128)} %stack.2), calls=%async_computation.6 | async-start | bytes 262144 | tf_op jit(solution)/shard_map/all_to_all | solution.py:35
  106.3 12.2 %all-to-all-start.4 = ((bf16[8,2,192]{2,1,0:T(2,128)(2,1)}), bf16[8,2,192]{2,1,0:T(2,128)(2,1)S(1)}, u32[]{:S(2)}, u32[]{:S(2)}) async-start(bf16[8,2,192]{2,1,0:T(2,128)(2,1)} %reshape.130), calls=%async_computation.4 | async-start | bytes 16384 | tf_op jit(solution)/shard_map/all_to_all | solution.py:153
  109.7 3.3 %copy-start.3 = (bf16[1024,384]{0,1:T(8,128)(2,1)S(1)}, bf16[1024,384]{0,1:T(8,128)(2,1)}, u32[]{:S(2)}) copy-start(bf16[1024,384]{0,1:T(8,128)(2,1)} %copy.131) | copy-start | bytes 2359300
  111.9 1.2 copy-start.1
  118.5 19.2 %all-to-all-start.7 = ((f32[32,8,384]{2,1,0:T(8,128)}), f32[32,8,384]{2,1,0:T(8,128)S(1)}, u32[]{:S(2)}, u32[]{:S(2)}) async-start(f32[32,8,384]{2,1,0:T(8,128)} %mul.66), calls=%async_computation.7 | async-start | bytes 786432 | tf_op jit(solution)/shard_map/all_to_all | solution.py:25
  124.3 1.6 %copy-start.2 = (bf16[3,256,1024]{2,1,0:T(8,128)(2,1)S(1)}, bf16[3,256,1024]{2,1,0:T(8,128)(2,1)}, u32[]{:S(2)}) copy-start(bf16[3,256,1024]{2,1,0:T(8,128)(2,1)} %copy-done.1) | copy-start | bytes 4718596
  124.3 1.6 %copy-start.6 = (bf16[32,8,384]{2,1,0:T(8,128)(2,1)S(1)}, bf16[32,8,384]{2,1,0:T(8,128)(2,1)}, u32[]{:S(2)}) copy-start(bf16[32,8,384]{2,1,0:T(8,128)(2,1)} %copy-done.5) | copy-start | bytes 589828
  125.9 19.4 %copy-start.4 = (bf16[3,32,8,1024]{3,2,1,0:T(8,128)(2,1)S(1)}, bf16[3,32,8,1024]{3,2,1,0:T(8,128)(2,1)}, u32[]{:S(2)}) copy-start(bf16[3,32,8,1024]{3,2,1,0:T(8,128)(2,1)} %fusion.4) | copy-start | bytes 4718596
  125.9 19.4 %copy-start.7 = (bf16[32,8,384]{2,1,0:T(8,128)(2,1)S(1)}, bf16[32,8,384]{2,1,0:T(8,128)(2,1)}, u32[]{:S(2)}) copy-start(bf16[32,8,384]{2,1,0:T(8,128)(2,1)} %copy.184) | copy-start | bytes 589828
  139.0 15.3 %all-to-all-start.8 = ((bf16[8,2,192]{2,1,0:T(2,128)(2,1)}), bf16[8,2,192]{2,1,0:T(2,128)(2,1)S(1)}, u32[]{:S(2)}, u32[]{:S(2)}) async-start(bf16[8,2,192]{2,1,0:T(2,128)(2,1)} %reshape.132), calls=%async_computation.8 | async-start | bytes 16384 | tf_op jit(solution)/shard_map/all_to_all | solution.py:154
  149.4 1.5 copy-start.8
